TPU v7x, 32 devices: a whole 2x2x4 slice. The times are simulated.
32 devices in a mesh: dp: 4 (over z), tensor: 8 (over y, x, core).
Axes of the slice: x: 2, y: 2, z: 4, core: 2. Of those that a mesh axis runs over, the one named last changes fastest.
Arguments:
- embed_rows: bfloat16 [98304, 512], P('tensor', 'dp'), may hold values from -6 to 6
- head_rows: bfloat16 [98304, 512], P('tensor', 'dp'), may hold values from -6 to 6
- row_offsets: int32 [2, 9], replicated, may hold values from -2047 to 67583, as said below
- slot_table: int32 [1024], replicated, may hold values from 0 to 1023, as said below
- probe: bfloat16 [512, 1024], replicated, may hold values from -0.25 to 0.25
Outputs:
- stored: bfloat16 [1024, 128, 512], P(('dp', 'tensor'))
- sketch: float32 [1024, 128, 1024], P(('dp', 'tensor'))
Inputs may be any that keep to these rules, and one draw needn't show every extreme that they name: row_offsets[m, 8] is row_offsets[m, 0] + 65536; every entry row_offsets[m, t] with t < 8 lies strictly within 2048 rows of t * 8192, and the distance 8192 // 4 - 1 is reached above and below among ranks 1 onward in every row of every draw; row_offsets[m, 0] is never 0, above 0 for one matrix and below 0 for the other. `slot_table`: A permutation of the 1024 block numbers. Devices along dp+tensor write 32 consecutive slots each; among one device's slots exactly 4 blocks come from each aligned range of 8192 vocabulary rows (rows t * 8192 onward of either matrix, both matrices together).
All inputs are finite; a program needn't handle non-finite values.
Results may differ from a plain program's by a relative error of at most 0.001.
Values may be sent and summed in bfloat16 or wider, within the bound.
A program may use at most 64 MiB of HBM per device.

v0:
```python
import jax
import jax.numpy as jnp
from jax import lax
from jax.sharding import PartitionSpec as P

R = 8192
BLOCK = 128


def from_behind(block, axis, distance):
    devices = range(lax.axis_size(axis))
    route = [((i - distance) % len(devices), i) for i in devices]
    return lax.ppermute(block, axis, route)


def shards(embed_rows, head_rows, row_offsets, slot_table, probe):
    n_tensor = lax.axis_size("tensor")
    n_data = lax.axis_size("dp")
    my_tensor = lax.axis_index("tensor")
    my_data = lax.axis_index("dp")
    quarter = R // 4
    height = embed_rows.shape[0]
    col_width = embed_rows.shape[1]
    buffers = [embed_rows, head_rows]
    own_start = row_offsets[:, my_tensor]
    next_start = row_offsets[:, my_tensor + 1]
    lead_part = jnp.stack([embed_rows[:quarter], head_rows[:quarter]])
    tail_begin = jnp.clip((my_tensor + 1) * R - own_start, 0, height - quarter)
    trail_part = jnp.stack(
        [lax.dynamic_slice_in_dim(buffers[m], tail_begin[m], quarter, 0) for m in range(2)]
    )
    from_right = from_behind(lead_part, "tensor", -1)
    from_left = from_behind(trail_part, "tensor", 1)
    local_row = jnp.arange(R, dtype=jnp.int32)[:, None]
    filler = jnp.zeros((R - quarter, col_width), embed_rows.dtype)
    aligned_list = []
    for m in range(2):
        extended = jnp.concatenate([from_left[m], buffers[m], from_right[m]], axis=0)
        before = own_start[m] - my_tensor * R
        after = next_start[m] - my_tensor * R
        middle = lax.dynamic_slice_in_dim(extended, quarter - before, R, 0)
        beyond = lax.dynamic_slice_in_dim(extended, quarter + height - after, R, 0)
        leading = jnp.concatenate([from_left[m], filler], axis=0)
        aligned_list.append(
            jnp.where(local_row < before, leading, jnp.where(local_row < after, middle, beyond))
        )
    aligned = jnp.stack(aligned_list)
    blocks = aligned.reshape(2 * (R // BLOCK), BLOCK, col_width)
    devices = n_tensor * n_data
    per_rank = R // BLOCK
    total_blocks = per_rank * n_tensor
    slot_count = 2 * total_blocks // devices
    max_from = slot_count // n_tensor
    slot_grid = slot_table.reshape(devices, slot_count)
    source = slot_grid % total_blocks // per_rank
    local_block = slot_grid // total_blocks * per_rank + slot_grid % per_rank
    from_me = source == my_tensor
    rank_order = jnp.cumsum(from_me.astype(jnp.int32), axis=1) - 1
    slot_index = jnp.arange(max_from, dtype=jnp.int32)
    select = from_me[:, None, :] & (rank_order[:, None, :] == slot_index[None, :, None])
    picked = jnp.sum(jnp.where(select, local_block[:, None, :], 0), axis=2).reshape(-1)
    outgoing = blocks[picked]
    incoming = lax.all_to_all(outgoing, ("dp", "tensor"), split_axis=0, concat_axis=0, tiled=True)
    writer = my_data * n_tensor + my_tensor
    my_source = source[writer]
    slot_range = jnp.arange(slot_count, dtype=jnp.int32)
    earlier = (my_source[None, :] == my_source[:, None]) & (
        slot_range[None, :] < slot_range[:, None]
    )
    rank_within = jnp.sum(earlier.astype(jnp.int32), axis=1)
    data_range = jnp.arange(n_data, dtype=jnp.int32)
    position = (data_range[None, :] * n_tensor + my_source[:, None]) * max_from + rank_within[
        :, None
    ]
    gathered = incoming[position]
    stored = gathered.transpose(0, 2, 1, 3).reshape(slot_count, BLOCK, n_data * col_width)
    sketch = jnp.dot(
        stored.reshape(slot_count * BLOCK, n_data * col_width),
        probe,
        preferred_element_type=jnp.float32,
    ).reshape(slot_count, BLOCK, probe.shape[1])
    return (stored, sketch)


def solution(mesh):
    return jax.shard_map(
        shards,
        mesh=mesh,
        in_specs=(P("tensor", "dp"), P("tensor", "dp"), P(), P(), P()),
        out_specs=(P(("dp", "tensor"), None, None), P(("dp", "tensor"), None, None)),
        check_vma=False,
    )
```

profile of v0, /device:TPU:0, one launch (start us, length us, event | category | flops | bytes accessed | tf_op | source)
XLA Modules:
  0.0 208.2 jit_solution(8664068044040684529)
XLA Ops:
  0.7 0.9 subtract_clamp_fusion
  1.5 0.5 fusion.16
  5.9 1.8 dynamic-slice_bitcast_fusion
  7.7 1.1 pad_maximum_fusion.4
  8.8 3.4 %collective-permute-start.1 = (bf16[2,2048,128]{2,1,0:T(8,128)(2,1)}, bf16[2,2048,128]{2,1,0:T(8,128)(2,1)S(1)}, u32[]{:S(2)}, u32[]{:S(2)}) collective-permute-start(bf16[2,2048,128]{2,1,0:T(8,128)(2,1)} %pad_maximum_fusion.4), channel_id=1, source_target_pairs={{1,0},{2,1},{3,2},{4,3},{5,4},{6,5},{7,6},{0,7},{9,8},{10,9},{11,1... | collective-permute-start | bytes 3145736 | tf_op jit(solution)/shard_map/ppermute | solution.py:13
  12.2 1.1 pad_maximum_fusion.3
  13.2 0.6 fusion.14
  16.5 0.2 reduce_window_sum.11
  16.7 0.1 select_reduce_fusion
  17.2 18.8 %collective-permute-done.1 = bf16[2,2048,128]{2,1,0:T(8,128)(2,1)S(1)} collective-permute-done((bf16[2,2048,128]{2,1,0:T(8,128)(2,1)}, bf16[2,2048,128]{2,1,0:T(8,128)(2,1)S(1)}, u32[]{:S(2)}, u32[]{:S(2)}) %collective-permute-start.1) | collective-permute-done | bytes 1048608 | tf_op jit(solution)/shard_map/ppermute | solution.py:13
  36.0 0.9 collective-permute-done
  37.0 13.4 %pad_maximum_fusion = bf16[16384,128]{1,0:T(8,128)(2,1)S(1)} fusion(bf16[2048,128]{1,0:T(8,128)(2,1)S(1)} %get-tuple-element.17, bf16[12288,128]{1,0:T(8,128)(2,1)S(1)} %copy-done.1, bf16[2048,128]{1,0:T(8,128)(2,1)S(1)} %get-tuple-element.15), kind=kLoop, calls=%fused_computation.2 | loop fusion | flops 12582912 | bytes 8388608 | tf_op jit(solution)/shard_map/concatenate | solution.py:38
  50.5 13.6 %pad_maximum_fusion.1 = bf16[16384,128]{1,0:T(8,128)(2,1)S(1)} fusion(bf16[2048,128]{1,0:T(8,128)(2,1)S(1)} %get-tuple-element.18, bf16[12288,128]{1,0:T(8,128)(2,1)S(1)} %copy-done.2, bf16[2048,128]{1,0:T(8,128)(2,1)S(1)} %get-tuple-element.16), kind=kLoop, calls=%fused_computation.3 | loop fusion | flops 12582912 | bytes 8388608 | tf_op jit(solution)/shard_map/concatenate | solution.py:38
  64.1 4.2 %select_bitcast_fusion.1 = bf16[1,8192,128]{2,1,0:T(8,128)(2,1)S(1)} fusion(bf16[16384,128]{1,0:T(8,128)(2,1)S(1)} %pad_maximum_fusion, s32[]{:T(128)S(6)} %select_n.112, s32[]{:T(128)S(6)} %select_n.111, bf16[2048,128]{1,0:T(8,128)(2,1)S(1)} %get-tuple-element.15, pred[8192]{0:T(1024)(128)(4,1)S(1)} %iota_compare_fusion.3, ...), kind=kLoop, calls=%fused_computation.6 | loop fusion | flops 2097152 | bytes 6832136 | tf_op jit(solution)/shard_map/stack | solution.py:47
  68.3 4.2 %select_bitcast_fusion = bf16[1,8192,128]{2,1,0:T(8,128)(2,1)S(1)} fusion(bf16[16384,128]{1,0:T(8,128)(2,1)S(1)} %pad_maximum_fusion.1, s32[]{:T(128)S(6)} %select_n.116, s32[]{:T(128)S(6)} %select_n.115, bf16[2048,128]{1,0:T(8,128)(2,1)S(1)} %get-tuple-element.16, pred[8192]{0:T(1024)(128)(4,1)S(1)} %iota_compare_fusion.1, ...), kind=kLoop, calls=%fused_computation.5 | loop fusion | flops 2097152 | bytes 6832136 | tf_op jit(solution)/shard_map/stack | solution.py:47
  72.5 2.4 %pad_maximum_fusion.2 = bf16[2,8192,128]{2,1,0:T(8,128)(2,1)} fusion(bf16[1,8192,128]{2,1,0:T(8,128)(2,1)S(1)} %select_bitcast_fusion, bf16[1,8192,128]{2,1,0:T(8,128)(2,1)S(1)} %select_bitcast_fusion.1), kind=kLoop, calls=%fused_computation.4 | loop fusion | flops 2097152 | bytes 8388608 | tf_op jit(solution)/shard_map/stack | solution.py:47
  74.9 5.3 %gather_fusion = bf16[128,128,128]{2,1,0:T(8,128)(2,1)} fusion(bf16[128,128,128]{2,1,0:T(8,128)(2,1)} %bitcast.43, s32[1024]{0:T(1024)S(1)} %pad_clamp_fusion.1), kind=kCustom, calls=%fused_computation | custom fusion | bytes 8389120 | tf_op jit(solution)/shard_map/gather | solution.py:62
  80.2 5.5 %all-to-all-start = ((bf16[128,128,128]{2,1,0:T(8,128)(2,1)}), bf16[128,128,128]{2,1,0:T(8,128)(2,1)}, u32[]{:S(2)}, u32[]{:S(2)}) async-start(bf16[128,128,128]{2,1,0:T(8,128)(2,1)} %gather_fusion), calls=%async_computation | async-start | bytes 8388608 | tf_op jit(solution)/shard_map/all_to_all | solution.py:63
  85.8 0.2 convert_reduce_fusion
  86.2 93.3 %all-to-all-done = bf16[128,128,128]{2,1,0:T(8,128)(2,1)} async-done(((bf16[128,128,128]{2,1,0:T(8,128)(2,1)}), bf16[128,128,128]{2,1,0:T(8,128)(2,1)}, u32[]{:S(2)}, u32[]{:S(2)}) %all-to-all-start) | async-done | bytes 4194336 | tf_op jit(solution)/shard_map/all_to_all | solution.py:63
  179.4 5.3 %gather_fusion.1 = bf16[128,128,128]{2,1,0:T(8,128)(2,1)} fusion(bf16[128,128,128]{2,1,0:T(8,128)(2,1)} %all-to-all-done, s32[1024]{0:T(1024)S(1)} %pad_clamp_fusion), kind=kCustom, calls=%fused_computation.1 | custom fusion | bytes 8389120 | tf_op jit(solution)/shard_map/gather | solution.py:75
  184.7 6.4 %copy.11 = bf16[32,128,4,128]{1,3,2,0:T(8,128)(2,1)} copy(bf16[32,128,4,128]{3,1,2,0:T(8,128)(2,1)} %bitcast.44) | data formatting | bytes 8388608 | tf_op jit(solution)/shard_map/transpose | solution.py:76
  191.1 6.4 %copy.13 = bf16[32,128,512]{2,1,0:T(8,128)(2,1)} copy(bf16[32,128,512]{1,2,0:T(8,128)(2,1)} %bitcast.41) | data formatting | bytes 8388608
  197.5 10.7 %fusion = f32[32,128,1024]{2,1,0:T(8,128)} fusion(bf16[32,128,512]{1,2,0:T(8,128)(2,1)} %bitcast.42, bf16[512,1024]{1,0:T(8,128)(2,1)S(1)} %copy-done), kind=kOutput, calls=%fused_computation.9 | convolution fusion | flops 4294967296 | bytes 22020096 | tf_op jit(solution)/shard_map/dot_general | solution.py:77
  (27 shorter events, 0.8 us)
Async XLA Ops:
  0.6 196.9 %copy-start = (bf16[512,1024]{1,0:T(8,128)(2,1)S(1)}, bf16[512,1024]{1,0:T(8,128)(2,1)}, u32[]{:S(2)}) copy-start(bf16[512,1024]{1,0:T(8,128)(2,1)} %param.9) | copy-start | bytes 3145732
  5.9 10.4 %copy-start.3 = (s32[1024]{0:T(1024)S(1)}, s32[1024]{0:T(1024)}, u32[]{:S(2)}) copy-start(s32[1024]{0:T(1024)} %param.8) | copy-start | bytes 12292
  8.8 27.1 %collective-permute-start.1 = (bf16[2,2048,128]{2,1,0:T(8,128)(2,1)}, bf16[2,2048,128]{2,1,0:T(8,128)(2,1)S(1)}, u32[]{:S(2)}, u32[]{:S(2)}) collective-permute-start(bf16[2,2048,128]{2,1,0:T(8,128)(2,1)} %pad_maximum_fusion.4), channel_id=1, source_target_pairs={{1,0},{2,1},{3,2},{4,3},{5,4},{6,5},{7,6},{0,7},{9,8},{10,9},{11,1... | collective-permute-start | bytes 3145736 | tf_op jit(solution)/shard_map/ppermute | solution.py:13
  13.2 23.7 %collective-permute-start = (bf16[2,2048,128]{2,1,0:T(8,128)(2,1)}, bf16[2,2048,128]{2,1,0:T(8,128)(2,1)S(1)}, u32[]{:S(2)}, u32[]{:S(2)}) collective-permute-start(bf16[2,2048,128]{2,1,0:T(8,128)(2,1)} %pad_maximum_fusion.3), channel_id=1, source_target_pairs={{7,0},{0,1},{1,2},{2,3},{3,4},{4,5},{5,6},{6,7},{15,8},{8,9},{9,10... | collective-permute-start | bytes 3145736 | tf_op jit(solution)/shard_map/ppermute | solution.py:13
  17.1 20.0 %copy-start.1 = (bf16[12288,128]{1,0:T(8,128)(2,1)S(1)}, bf16[12288,128]{1,0:T(8,128)(2,1)}, u32[]{:S(2)}) copy-start(bf16[12288,128]{1,0:T(8,128)(2,1)} %param.5) | copy-start | bytes 9437188
  37.0 13.4 %copy-start.2 = (bf16[12288,128]{1,0:T(8,128)(2,1)S(1)}, bf16[12288,128]{1,0:T(8,128)(2,1)}, u32[]{:S(2)}) copy-start(bf16[12288,128]{1,0:T(8,128)(2,1)} %param.6) | copy-start | bytes 9437188
  80.2 99.2 %all-to-all-start = ((bf16[128,128,128]{2,1,0:T(8,128)(2,1)}), bf16[128,128,128]{2,1,0:T(8,128)(2,1)}, u32[]{:S(2)}, u32[]{:S(2)}) async-start(bf16[128,128,128]{2,1,0:T(8,128)(2,1)} %gather_fusion), calls=%async_computation | async-start | bytes 8388608 | tf_op jit(solution)/shard_map/all_to_all | solution.py:63
where the time goes:
time: 209 us; the launch traced here: 208 us
  waiting for transfers between devices  113 us (54%)
  other arithmetic  41.5 us (20%)
  local copies, waits for them, and re-layouts  26.9 us (13%)
  matrix products  10.7 us (5%)
  starting transfers between devices  8.89 us (4%)
  between operations  7.29 us (3%)
    all_to_all x1, waiting for transfers between devices, shards(): lax.all_to_all(outgoing, ('dp', 'tensor'), split_axis=0, concat_axis=0, t...  93.3 us
    concatenate x2, other arithmetic, shards(): jnp.concatenate([from_left[m], buffers[m], from_right[m]], axis=0)  27 us
    ppermute x2, waiting for transfers between devices, from_behind(): return lax.ppermute(block, axis, route)  19.7 us
    another operation x3, other arithmetic, shards(): aligned = jnp.stack(aligned_list)  10.8 us
    dot_general x1, matrix products, shards(): jnp.dot(stored.reshape(slot_count * BLOCK, n_data * col_width), probe, pr...  10.7 us
    unnamed x9, local copies, waits for them, and re-layouts  6.44 us
    transpose x1, local copies, waits for them, and re-layouts, shards(): gathered.transpose(0, 2, 1, 3)  6.41 us
    all_to_all x1, starting transfers between devices, shards(): lax.all_to_all(outgoing, ('dp', 'tensor'), split_axis=0, concat_axis=0, t...  5.53 us
  transfers between devices with their start and end apart: 3, of which 3 were waited for; matrix products, arithmetic and copies ran while one was open for 1% of the time, Pallas kernels for 0%

commit v1 on v0

v1 whole, which is shorter than its diff:
```python
import functools

import jax
import jax.numpy as jnp
from jax import lax
from jax.experimental import pallas as pl
from jax.experimental.pallas import tpu as pltpu
from jax.sharding import PartitionSpec as P

R = 8192
BLOCK = 128
TILE = 16
WINDOW = 256
MIB = 1 << 20


def from_behind(block, axis, distance):
    devices = range(lax.axis_size(axis))
    route = [((i - distance) % len(devices), i) for i in devices]
    return lax.ppermute(block, axis, route)


def floor_tile(value):
    return lax.shift_left(lax.shift_right_arithmetic(value, 4), 4)


def edges_kernel(begin_ref, embed_ref, head_ref, lead_ref, trail_ref, sems):
    copies = []
    for m, buffer in enumerate((embed_ref, head_ref)):
        begin = pl.multiple_of(begin_ref[m], TILE)
        copies.append(
            pltpu.make_async_copy(buffer.at[pl.ds(0, lead_ref.shape[1])], lead_ref.at[m], sems.at[2 * m])
        )
        copies.append(
            pltpu.make_async_copy(
                buffer.at[pl.ds(begin, trail_ref.shape[1])], trail_ref.at[m], sems.at[2 * m + 1]
            )
        )
    for copy in copies:
        copy.start()
    for copy in copies:
        copy.wait()


def pack_kernel(per_rank, per_step, picked_ref, meta_ref, embed_ref, head_ref, left_ref, right_ref,
                out_ref, rows, edge, sems):
    height = embed_ref.shape[0]
    left_rows, right_rows = left_ref.shape[1], right_ref.shape[1]
    step = pl.program_id(0)

    @pl.when(step == 0)
    def _():
        copies = []
        for m, buffer in enumerate((embed_ref, head_ref)):
            copies.append(
                pltpu.make_async_copy(buffer, rows.at[pl.ds(m * height, height)], sems.at[3 * m])
            )
            copies.append(
                pltpu.make_async_copy(
                    left_ref.at[m], edge.at[pl.ds(m * left_rows, left_rows)], sems.at[3 * m + 1]
                )
            )
            copies.append(
                pltpu.make_async_copy(
                    right_ref.at[m],
                    edge.at[pl.ds(2 * left_rows + m * right_rows, right_rows)],
                    sems.at[3 * m + 2],
                )
            )
        for copy in copies:
            copy.start()
        for copy in copies:
            copy.wait()

    row = lax.broadcasted_iota(jnp.int32, (BLOCK, WINDOW), 0)
    ahead = lax.broadcasted_iota(jnp.int32, (BLOCK, WINDOW), 1) - row

    def place(offset, low, high, window):
        chosen = (ahead == offset) & (row >= low) & (row < high)
        selector = jnp.where(chosen, 1.0, 0.0).astype(jnp.bfloat16)
        return jnp.dot(selector, window, preferred_element_type=jnp.float32).astype(jnp.bfloat16)

    for q in range(per_step):
        block = picked_ref[step * per_step + q]
        m = (block >= per_rank).astype(jnp.int32)
        first = (block - m * per_rank) * BLOCK
        before, after, skew = meta_ref[m, 0], meta_ref[m, 1], meta_ref[m, 2]
        start = first - before
        base = jnp.clip(floor_tile(start), 0, height - WINDOW)
        window = rows[pl.ds(pl.multiple_of(m * height + base, TILE), WINDOW), :]
        out_ref[q] = place(start - base, before - first, after - first, window)

        @pl.when((first < before) | (first + BLOCK > after))
        def _():
            is_left = first < before
            begin = jnp.where(is_left, first + skew, first - after)
            limit = jnp.where(is_left, left_rows, right_rows) - WINDOW
            part = jnp.where(is_left, m * left_rows, 2 * left_rows + m * right_rows)
            base = jnp.clip(floor_tile(begin), 0, limit)
            window = edge[pl.ds(pl.multiple_of(part + base, TILE), WINDOW), :]
            low = jnp.where(is_left, 0, after - first)
            high = jnp.where(is_left, before - first, BLOCK)
            out_ref[q] = out_ref[q] + place(begin - base, low, high, window)


def finish_kernel(n_data, per_step, position_ref, incoming_ref, probe_ref, stored_ref, sketch_ref):
    width = incoming_ref.shape[2]
    step = pl.program_id(0)
    for q in range(per_step):
        for d in range(n_data):
            where = position_ref[(step * per_step + q) * n_data + d]
            stored_ref[q, :, d * width : (d + 1) * width] = incoming_ref[where]
        sketch_ref[q] = jnp.dot(
            stored_ref[q], probe_ref[...], preferred_element_type=jnp.float32
        )


def edges(begin, embed_rows, head_rows, quarter):
    width = embed_rows.shape[1]
    kind = embed_rows.dtype
    whole = pl.BlockSpec(memory_space=pltpu.VMEM)
    return pl.pallas_call(
        edges_kernel,
        grid_spec=pltpu.PrefetchScalarGridSpec(
            num_scalar_prefetch=1,
            grid=(),
            in_specs=[pl.BlockSpec(memory_space=pl.ANY)] * 2,
            out_specs=[whole, whole],
            scratch_shapes=[pltpu.SemaphoreType.DMA((4,))],
        ),
        out_shape=[
            jax.ShapeDtypeStruct((2, quarter, width), kind),
            jax.ShapeDtypeStruct((2, quarter + TILE, width), kind),
        ],
        name="edges",
    )(begin, embed_rows, head_rows)


def pack(picked, meta, embed_rows, head_rows, from_left, from_right):
    height, width = embed_rows.shape
    count = picked.shape[0]
    per_step = 16
    kind = embed_rows.dtype
    return pl.pallas_call(
        functools.partial(pack_kernel, R // BLOCK, per_step),
        grid_spec=pltpu.PrefetchScalarGridSpec(
            num_scalar_prefetch=2,
            grid=(count // per_step,),
            in_specs=[pl.BlockSpec(memory_space=pl.ANY)] * 4,
            out_specs=pl.BlockSpec((per_step, BLOCK, width), lambda i, *_: (i, 0, 0)),
            scratch_shapes=[
                pltpu.VMEM((2 * height, width), kind),
                pltpu.VMEM((2 * (from_left.shape[1] + from_right.shape[1]), width), kind),
                pltpu.SemaphoreType.DMA((6,)),
            ],
        ),
        out_shape=jax.ShapeDtypeStruct((count, BLOCK, width), kind),
        compiler_params=pltpu.CompilerParams(dimension_semantics=("arbitrary",)),
        name="pack",
    )(picked, meta, embed_rows, head_rows, from_left, from_right)


def finish(position, incoming, probe, slot_count, n_data):
    width = incoming.shape[2]
    columns, sketch_width = probe.shape
    per_step = 4
    return pl.pallas_call(
        functools.partial(finish_kernel, n_data, per_step),
        grid_spec=pltpu.PrefetchScalarGridSpec(
            num_scalar_prefetch=1,
            grid=(slot_count // per_step,),
            in_specs=[
                pl.BlockSpec(incoming.shape, lambda i, *_: (0, 0, 0)),
                pl.BlockSpec(probe.shape, lambda i, *_: (0, 0)),
            ],
            out_specs=[
                pl.BlockSpec((per_step, BLOCK, columns), lambda i, *_: (i, 0, 0)),
                pl.BlockSpec((per_step, BLOCK, sketch_width), lambda i, *_: (i, 0, 0)),
            ],
        ),
        out_shape=[
            jax.ShapeDtypeStruct((slot_count, BLOCK, columns), incoming.dtype),
            jax.ShapeDtypeStruct((slot_count, BLOCK, sketch_width), jnp.float32),
        ],
        compiler_params=pltpu.CompilerParams(
            dimension_semantics=("arbitrary",), vmem_limit_bytes=48 * MIB
        ),
        name="finish",
    )(position, incoming, probe)


def shards(embed_rows, head_rows, row_offsets, slot_table, probe):
    n_tensor = lax.axis_size("tensor")
    n_data = lax.axis_size("dp")
    my_tensor = lax.axis_index("tensor")
    my_data = lax.axis_index("dp")
    quarter = R // 4
    height = embed_rows.shape[0]

    def tail_begin(rank):
        return jnp.clip((rank + 1) * R - row_offsets[:, rank], 0, height - quarter - 1)

    begin = floor_tile(tail_begin(my_tensor))
    lead_part, trail_part = edges(begin, embed_rows, head_rows, quarter)
    from_left = from_behind(trail_part, "tensor", 1)
    from_right = from_behind(lead_part, "tensor", -1)
    left_begin = tail_begin((my_tensor + n_tensor - 1) % n_tensor)
    skew = left_begin - floor_tile(left_begin)
    meta = jnp.stack(
        [row_offsets[:, my_tensor] - my_tensor * R, row_offsets[:, my_tensor + 1] - my_tensor * R, skew], axis=1
    )

    devices = n_tensor * n_data
    per_rank = R // BLOCK
    total_blocks = per_rank * n_tensor
    slot_count = 2 * total_blocks // devices
    max_from = slot_count // n_tensor
    slot_grid = slot_table.reshape(devices, slot_count)
    source = slot_grid % total_blocks // per_rank
    local_block = slot_grid // total_blocks * per_rank + slot_grid % per_rank
    from_me = source == my_tensor
    slot_range = jnp.arange(slot_count, dtype=jnp.int32)
    lower = slot_range[None, :] < slot_range[:, None]
    rank_order = jnp.sum((from_me[:, None, :] & lower[None]).astype(jnp.int32), axis=2)
    slot_index = jnp.arange(max_from, dtype=jnp.int32)
    select = from_me[:, None, :] & (rank_order[:, None, :] == slot_index[None, :, None])
    picked = jnp.sum(jnp.where(select, local_block[:, None, :], 0), axis=2).reshape(-1)
    writer = my_data * n_tensor + my_tensor
    my_source = source[writer]
    earlier = (my_source[None, :] == my_source[:, None]) & lower
    rank_within = jnp.sum(earlier.astype(jnp.int32), axis=1)
    data_range = jnp.arange(n_data, dtype=jnp.int32)
    position = (
        (data_range[None, :] * n_tensor + my_source[:, None]) * max_from + rank_within[:, None]
    ).reshape(-1)

    outgoing = pack(picked, meta, embed_rows, head_rows, from_left, from_right)
    incoming = lax.all_to_all(outgoing, ("dp", "tensor"), split_axis=0, concat_axis=0, tiled=True)
    stored, sketch = finish(position, incoming, probe, slot_count, n_data)
    return (stored, sketch)


def solution(mesh):
    return jax.shard_map(
        shards,
        mesh=mesh,
        in_specs=(P("tensor", "dp"), P("tensor", "dp"), P(), P(), P()),
        out_specs=(P(("dp", "tensor"), None, None), P(("dp", "tensor"), None, None)),
        check_vma=False,
    )
```

time: 209 us -> 180 us (0.86)
  Pallas kernels: 0 us -> 43.6 us
  other arithmetic: 41.5 us -> 3.31 us
  local copies, waits for them, and re-layouts: 26.9 us -> 2.88 us
  matrix products: 10.7 us -> 0 us
  between operations: 7.29 us -> 0.74 us
  starting transfers between devices: 8.89 us -> 14.1 us
    pallas_call x0 -> x3, Pallas kernels: none -> 43.6 us  [the longest x1 28.3 us: pack(): pl.pallas_call(functools.partial(pack_kernel, R // BLOCK, per_step), grid...]
    concatenate x2 -> x0, other arithmetic: 27 us -> none  [shards(): jnp.concatenate([from_left[m], buffers[m], from_right[m]], axis=0)]
    another operation x6 -> x1, other arithmetic: 13.1 us -> 0.66 us  [shards(): jnp.stack([row_offsets[:, my_tensor] - my_tensor * R, row_offsets[:, my_t...]
    dot_general x1 -> x0, matrix products: 10.7 us -> none  [shards(): jnp.dot(stored.reshape(slot_count * BLOCK, n_data * col_width), probe, pr...]
    gather x2 -> x0, local copies, waits for them, and re-layouts: 10.6 us -> none  [the longest x1 5.28 us: shards(): gathered = incoming[position]]
    transpose x1 -> x0, local copies, waits for them, and re-layouts: 6.41 us -> none  [shards(): gathered.transpose(0, 2, 1, 3)]
    all_to_all x1, starting transfers between devices: 5.53 us -> 10.6 us  [shards(): lax.all_to_all(outgoing, ('dp', 'tensor'), split_axis=0, concat_axis=0, t...]
    unnamed x9 -> x8, local copies, waits for them, and re-layouts: 6.44 us -> 1.97 us
  transfers between devices with their start and end apart: 3 -> 3, of which waited for: 3 -> 2; matrix products, arithmetic and copies ran while one was open for 1% -> 1% of each run, Pallas kernels for 0% -> 0%
where the time goes in v1:
time: 180 us; the launch traced here: 179 us
  waiting for transfers between devices  114 us (63%)
  Pallas kernels  43.6 us (24%)
  starting transfers between devices  14.1 us (8%)
  other arithmetic  3.31 us (2%)
  local copies, waits for them, and re-layouts  2.88 us (2%)
    all_to_all x1, waiting for transfers between devices, shards(): lax.all_to_all(outgoing, ('dp', 'tensor'), split_axis=0, concat_axis=0, t...  93.3 us
    pallas_call x1, Pallas kernels, pack(): pl.pallas_call(functools.partial(pack_kernel, R // BLOCK, per_step), grid...  28.3 us
    ppermute x2, waiting for transfers between devices, from_behind(): return lax.ppermute(block, axis, route)  20.6 us
    pallas_call x1, Pallas kernels, finish(): pl.pallas_call(functools.partial(finish_kernel, n_data, per_step), grid_s...  11.8 us
    all_to_all x1, starting transfers between devices, shards(): lax.all_to_all(outgoing, ('dp', 'tensor'), split_axis=0, concat_axis=0, t...  10.6 us
  transfers between devices with their start and end apart: 3, of which 2 were waited for; matrix products, arithmetic and copies ran while one was open for 1% of the time, Pallas kernels for 0%

profile of v1, /device:TPU:0, one launch (start us, length us, event | category | flops | bytes accessed | tf_op | source)
XLA Modules:
  0.0 178.6 jit_solution(12508022709059679742)
XLA Ops:
  0.6 0.0 copy-start.3
  0.7 1.6 shift-left_reduce_fusion
  2.2 3.5 %edges.1 = (bf16[2,2048,128]{2,1,0:T(8,128)(2,1)}, bf16[2,2064,128]{2,1,0:T(8,128)(2,1)}) custom-call(s32[2]{0:T(128)} %get-tuple-element.8.begin_ref, bf16[12288,128]{1,0:T(8,128)(2,1)} %embed_ref.3, bf16[12288,128]{1,0:T(8,128)(2,1)} %head_ref.3), custom_call_target="tpu_custom_call" | custom-call | tf_op jit(solution)/shard_map/edges/pallas_call | solution.py:122
  5.8 0.5 collective-permute-start
  6.3 2.9 %collective-permute-start.1 = (bf16[2,2048,128]{2,1,0:T(8,128)(2,1)}, bf16[2,2048,128]{2,1,0:T(8,128)(2,1)S(1)}, u32[]{:S(2)}, u32[]{:S(2)}) collective-permute-start(bf16[2,2048,128]{2,1,0:T(8,128)(2,1)} %get-tuple-element.5), channel_id=1, source_target_pairs={{1,0},{2,1},{3,2},{4,3},{5,4},{6,5},{7,6},{0,7},{9,8},{10,9},{11,1... | collective-permute-start | bytes 3145736 | tf_op jit(solution)/shard_map/ppermute | solution.py:20
  9.3 0.0 copy-done.3
  9.3 0.1 reshape.134
  9.4 0.6 convert_reduce_fusion
  10.0 0.1 select_reduce_fusion
  10.2 0.1 copy.7
  10.3 0.6 reshape.135.picked_ref
  10.9 0.7 pad_add_fusion.meta_ref
  11.5 20.6 %collective-permute-done.1.right_ref = bf16[2,2048,128]{2,1,0:T(8,128)(2,1)S(1)} collective-permute-done((bf16[2,2048,128]{2,1,0:T(8,128)(2,1)}, bf16[2,2048,128]{2,1,0:T(8,128)(2,1)S(1)}, u32[]{:S(2)}, u32[]{:S(2)}) %collective-permute-start.1) | collective-permute-done | bytes 1048608 | tf_op jit(solution)/shard_map/ppermute | solution.py:20
  32.2 0.0 collective-permute-done.left_ref
  32.2 1.0 copy-done.2
  33.2 1.0 copy-done.1
  34.1 28.3 %pack.1 = bf16[128,128,128]{2,1,0:T(8,128)(2,1)} custom-call(s32[128]{0:T(128)} %reshape.135.picked_ref, s32[2,3]{1,0:T(2,128)} %pad_add_fusion.meta_ref, bf16[12288,128]{1,0:T(8,128)(2,1)} %embed_ref.3, bf16[12288,128]{1,0:T(8,128)(2,1)} %head_ref.3, bf16[2,2064,128]{2,1,0:T(8,128)(2,1)} %copy-done.1, bf16[2,2048,128]{2,1,0:T(8,128)(2,1)} %copy-done.2), custom_call_target="tpu_custom_call" | custom-call | tf_op jit(solution)/shard_map/pack/pallas_call | solution.py:144
  62.4 0.0 copy-start
  62.4 10.6 %all-to-all-start = ((bf16[128,128,128]{2,1,0:T(8,128)(2,1)}), bf16[128,128,128]{2,1,0:T(8,128)(2,1)}, u32[]{:S(2)}, u32[]{:S(2)}) async-start(bf16[128,128,128]{2,1,0:T(8,128)(2,1)} %pack.1), calls=%async_computation | async-start | bytes 8388608 | tf_op jit(solution)/shard_map/all_to_all | solution.py:238
  73.1 0.2 convert_reduce_fusion.1
  73.3 0.1 multiply_add_fusion
  73.4 0.1 add.106.position_ref
  73.5 93.3 %all-to-all-done.incoming_ref = bf16[128,128,128]{2,1,0:T(8,128)(2,1)} async-done(((bf16[128,128,128]{2,1,0:T(8,128)(2,1)}), bf16[128,128,128]{2,1,0:T(8,128)(2,1)}, u32[]{:S(2)}, u32[]{:S(2)}) %all-to-all-start) | async-done | bytes 4194336 | tf_op jit(solution)/shard_map/all_to_all | solution.py:238
  166.8 11.8 %finish.1 = (bf16[32,128,512]{2,1,0:T(8,128)(2,1)}, f32[32,128,1024]{2,1,0:T(8,128)}) custom-call(s32[128]{0:T(128)S(1)} %add.106.position_ref, bf16[128,128,128]{2,1,0:T(8,128)(2,1)} %all-to-all-done.incoming_ref, bf16[512,1024]{1,0:T(8,128)(2,1)S(1)} %copy-done), custom_call_target="tpu_custom_call" | custom-call | tf_op jit(solution)/shard_map/finish/pallas_call | solution.py:167
  (7 shorter events, 0.1 us)
Async XLA Ops:
  0.6 8.6 %copy-start.3 = (s32[1024]{0:T(1024)S(1)}, s32[1024]{0:T(1024)}, u32[]{:S(2)}) copy-start(s32[1024]{0:T(1024)} %param.8) | copy-start | bytes 12292
  5.8 26.4 %collective-permute-start = (bf16[2,2064,128]{2,1,0:T(8,128)(2,1)}, bf16[2,2064,128]{2,1,0:T(8,128)(2,1)S(1)}, u32[]{:S(2)}, u32[]{:S(2)}) collective-permute-start(bf16[2,2064,128]{2,1,0:T(8,128)(2,1)} %get-tuple-element.4), channel_id=1, source_target_pairs={{7,0},{0,1},{1,2},{2,3},{3,4},{4,5},{5,6},{6,7},{15,8},{8,9},{9,10... | collective-permute-start | bytes 3170312 | tf_op jit(solution)/shard_map/ppermute | solution.py:20
  6.3 25.9 %collective-permute-start.1 = (bf16[2,2048,128]{2,1,0:T(8,128)(2,1)}, bf16[2,2048,128]{2,1,0:T(8,128)(2,1)S(1)}, u32[]{:S(2)}, u32[]{:S(2)}) collective-permute-start(bf16[2,2048,128]{2,1,0:T(8,128)(2,1)} %get-tuple-element.5), channel_id=1, source_target_pairs={{1,0},{2,1},{3,2},{4,3},{5,4},{6,5},{7,6},{0,7},{9,8},{10,9},{11,1... | collective-permute-start | bytes 3145736 | tf_op jit(solution)/shard_map/ppermute | solution.py:20
  32.2 1.0 copy-start.2
  33.2 1.0 copy-start.1
  62.4 104.3 %copy-start = (bf16[512,1024]{1,0:T(8,128)(2,1)S(1)}, bf16[512,1024]{1,0:T(8,128)(2,1)}, u32[]{:S(2)}) copy-start(bf16[512,1024]{1,0:T(8,128)(2,1)} %probe_ref.1) | copy-start | bytes 3145732
  62.4 104.3 %all-to-all-start = ((bf16[128,128,128]{2,1,0:T(8,128)(2,1)}), bf16[128,128,128]{2,1,0:T(8,128)(2,1)}, u32[]{:S(2)}, u32[]{:S(2)}) async-start(bf16[128,128,128]{2,1,0:T(8,128)(2,1)} %pack.1), calls=%async_computation | async-start | bytes 8388608 | tf_op jit(solution)/shard_map/all_to_all | solution.py:238

commit v2 on v1

v2 whole, which is shorter than its diff:
```python
import functools

import jax
import jax.numpy as jnp
from jax import lax
from jax.experimental import pallas as pl
from jax.experimental.pallas import tpu as pltpu
from jax.sharding import PartitionSpec as P

R = 8192
BLOCK = 128
TILE = 16
WINDOW = 256
MIB = 1 << 20


def from_behind(block, axis, distance):
    devices = range(lax.axis_size(axis))
    route = [((i - distance) % len(devices), i) for i in devices]
    return lax.ppermute(block, axis, route)


def floor_tile(value):
    return lax.shift_left(lax.shift_right_arithmetic(value, 4), 4)


def tail_begin(offset, rank, height, quarter):
    return jnp.clip((rank + 1) * R - offset, 0, height - quarter - 1)


def selector(offset):
    row = lax.broadcasted_iota(jnp.int32, (BLOCK, WINDOW), 0)
    column = lax.broadcasted_iota(jnp.int32, (BLOCK, WINDOW), 1)
    return jnp.where(column - row == offset, 1.0, 0.0).astype(jnp.bfloat16)


def place(offset, window):
    moved = jnp.dot(selector(offset), window, preferred_element_type=jnp.float32)
    return moved.astype(window.dtype)


def edges_kernel(offsets_ref, embed_ref, head_ref, lead_ref, trail_ref, sems):
    rank = lax.axis_index("tensor")
    copies = []
    for m, buffer in enumerate((embed_ref, head_ref)):
        begin = floor_tile(
            tail_begin(offsets_ref[m, rank], rank, buffer.shape[0], lead_ref.shape[1])
        )
        begin = pl.multiple_of(begin, TILE)
        copies.append(
            pltpu.make_async_copy(buffer.at[pl.ds(0, lead_ref.shape[1])], lead_ref.at[m], sems.at[2 * m])
        )
        copies.append(
            pltpu.make_async_copy(
                buffer.at[pl.ds(begin, trail_ref.shape[1])], trail_ref.at[m], sems.at[2 * m + 1]
            )
        )
    for copy in copies:
        copy.start()
    for copy in copies:
        copy.wait()


def pack_kernel(per_rank, per_step, picked_ref, meta_ref, embed_ref, head_ref, out_ref, rows, sems):
    height = embed_ref.shape[0]
    step = pl.program_id(0)

    @pl.when(step == 0)
    def _():
        copies = [
            pltpu.make_async_copy(buffer, rows.at[pl.ds(m * height, height)], sems.at[m])
            for m, buffer in enumerate((embed_ref, head_ref))
        ]
        for copy in copies:
            copy.start()
        for copy in copies:
            copy.wait()

    for q in range(per_step):
        block = picked_ref[step * per_step + q]
        m = (block >= per_rank).astype(jnp.int32)
        start = (block - m * per_rank) * BLOCK - meta_ref[m, 0]
        base = jnp.clip(floor_tile(start), 0, height - WINDOW)
        window = rows[pl.ds(pl.multiple_of(m * height + base, TILE), WINDOW), :]
        out_ref[q] = place(start - base, window)


def fix_kernel(per_rank, group, slots_ref, count_ref, picked_ref, meta_ref, packed_ref, left_ref, right_ref,
               out_ref, work, get_sems, put_sems):
    del packed_ref
    count = count_ref[0]

    def get(k):
        return pltpu.make_async_copy(out_ref.at[slots_ref[k]], work.at[k], get_sems.at[k])

    def put(k):
        return pltpu.make_async_copy(work.at[k], out_ref.at[slots_ref[k]], put_sems.at[k])

    def span(g):
        return g * group, jnp.minimum(count, (g + 1) * group)

    def start_get(k, carry):
        get(k).start()
        return carry

    def wait_get(k, carry):
        get(k).wait()
        return carry

    def start_put(k, carry):
        put(k).start()
        return carry

    def wait_put(k, carry):
        put(k).wait()
        return carry

    lax.fori_loop(0, count, start_get, 0)
    row = lax.broadcasted_iota(jnp.int32, (BLOCK, work.shape[2]), 0)

    def one_group(g, carry):
        low_k, high_k = span(g)
        lax.fori_loop(low_k, high_k, wait_get, 0)
        for q in range(group):
            k = g * group + q
            block = picked_ref[slots_ref[k]]
            m = (block >= per_rank).astype(jnp.int32)
            first = (block - m * per_rank) * BLOCK
            before, after, skew = meta_ref[m, 0], meta_ref[m, 1], meta_ref[m, 2]
            is_left = first < before
            left_base = jnp.clip(floor_tile(first + skew), 0, left_ref.shape[1] - WINDOW)
            right_base = jnp.clip(floor_tile(first - after), 0, right_ref.shape[1] - WINDOW)
            window = jnp.where(
                is_left,
                left_ref[m, pl.ds(pl.multiple_of(left_base, TILE), WINDOW), :],
                right_ref[m, pl.ds(pl.multiple_of(right_base, TILE), WINDOW), :],
            )
            offset = jnp.where(is_left, first + skew - left_base, first - after - right_base)
            low = jnp.where(is_left, 0, after - first)
            high = jnp.where(is_left, before - first, BLOCK)
            moved = jnp.dot(selector(offset), window, preferred_element_type=jnp.float32)
            kept = work[k].astype(jnp.float32)
            work[k] = jnp.where((row >= low) & (row < high), moved, kept).astype(work.dtype)
        lax.fori_loop(low_k, high_k, start_put, 0)
        return carry

    lax.fori_loop(0, (count + group - 1) // group, one_group, 0)
    lax.fori_loop(0, count, wait_put, 0)


def finish_kernel(n_data, per_step, position_ref, incoming_ref, probe_ref, stored_ref, sketch_ref, slots, sems):
    width = incoming_ref.shape[2]
    step = pl.program_id(0)
    steps = pl.num_programs(0)
    depth = slots.shape[0]

    def copies(s):
        place_of = lax.rem(s, depth)
        return [
            pltpu.make_async_copy(
                incoming_ref.at[position_ref[(s * per_step + q) * n_data + d]],
                slots.at[place_of, q, :, pl.ds(d * width, width)],
                sems.at[place_of, q * n_data + d],
            )
            for q in range(per_step)
            for d in range(n_data)
        ]

    @pl.when(step == 0)
    def _():
        for s in range(depth - 1):
            for copy in copies(s):
                copy.start()

    @pl.when(step + depth - 1 < steps)
    def _():
        for copy in copies(step + depth - 1):
            copy.start()

    for copy in copies(step):
        copy.wait()
    here = lax.rem(step, depth)
    for q in range(per_step):
        stored_ref[q] = slots[here, q]
        sketch_ref[q] = jnp.dot(slots[here, q], probe_ref[...], preferred_element_type=jnp.float32)


def edges(row_offsets, embed_rows, head_rows, quarter):
    width = embed_rows.shape[1]
    kind = embed_rows.dtype
    whole = pl.BlockSpec(memory_space=pltpu.VMEM)
    return pl.pallas_call(
        edges_kernel,
        grid_spec=pltpu.PrefetchScalarGridSpec(
            num_scalar_prefetch=1,
            grid=(),
            in_specs=[pl.BlockSpec(memory_space=pl.ANY)] * 2,
            out_specs=[whole, whole],
            scratch_shapes=[pltpu.SemaphoreType.DMA((4,))],
        ),
        out_shape=[
            jax.ShapeDtypeStruct((2, quarter, width), kind),
            jax.ShapeDtypeStruct((2, quarter + TILE, width), kind),
        ],
        name="edges",
    )(row_offsets, embed_rows, head_rows)


def pack(picked, meta, embed_rows, head_rows):
    height, width = embed_rows.shape
    count = picked.shape[0]
    per_step = 16
    kind = embed_rows.dtype
    return pl.pallas_call(
        functools.partial(pack_kernel, R // BLOCK, per_step),
        grid_spec=pltpu.PrefetchScalarGridSpec(
            num_scalar_prefetch=2,
            grid=(count // per_step,),
            in_specs=[pl.BlockSpec(memory_space=pl.ANY)] * 2,
            out_specs=pl.BlockSpec((per_step, BLOCK, width), lambda i, *_: (i, 0, 0)),
            scratch_shapes=[
                pltpu.VMEM((2 * height, width), kind),
                pltpu.SemaphoreType.DMA((2,)),
            ],
        ),
        out_shape=jax.ShapeDtypeStruct((count, BLOCK, width), kind),
        compiler_params=pltpu.CompilerParams(
            dimension_semantics=("arbitrary",), vmem_limit_bytes=24 * MIB
        ),
        cost_estimate=pl.CostEstimate(
            flops=2 * count * BLOCK * WINDOW * width, bytes_accessed=24 * MIB, transcendentals=0
        ),
        name="pack",
    )(picked, meta, embed_rows, head_rows)


def fix(slots, count, picked, meta, packed, from_left, from_right):
    most, group = slots.shape[0], 8
    return pl.pallas_call(
        functools.partial(fix_kernel, R // BLOCK, group),
        grid_spec=pltpu.PrefetchScalarGridSpec(
            num_scalar_prefetch=4,
            grid=(),
            in_specs=[
                pl.BlockSpec(memory_space=pltpu.HBM),
                pl.BlockSpec(memory_space=pltpu.VMEM),
                pl.BlockSpec(memory_space=pltpu.VMEM),
            ],
            out_specs=pl.BlockSpec(memory_space=pltpu.HBM),
            scratch_shapes=[
                pltpu.VMEM((most,) + packed.shape[1:], packed.dtype),
                pltpu.SemaphoreType.DMA((most,)),
                pltpu.SemaphoreType.DMA((most,)),
            ],
        ),
        out_shape=jax.ShapeDtypeStruct(packed.shape, packed.dtype),
        input_output_aliases={4: 0},
        compiler_params=pltpu.CompilerParams(vmem_limit_bytes=24 * MIB),
        name="fix",
    )(slots, count, picked, meta, packed, from_left, from_right)


def finish(position, incoming, probe, slot_count, n_data):
    columns, sketch_width = probe.shape
    per_step, depth = 2, 4
    return pl.pallas_call(
        functools.partial(finish_kernel, n_data, per_step),
        grid_spec=pltpu.PrefetchScalarGridSpec(
            num_scalar_prefetch=1,
            grid=(slot_count // per_step,),
            in_specs=[
                pl.BlockSpec(memory_space=pl.ANY),
                pl.BlockSpec(probe.shape, lambda i, *_: (0, 0)),
            ],
            out_specs=[
                pl.BlockSpec((per_step, BLOCK, columns), lambda i, *_: (i, 0, 0)),
                pl.BlockSpec((per_step, BLOCK, sketch_width), lambda i, *_: (i, 0, 0)),
            ],
            scratch_shapes=[
                pltpu.VMEM((depth, per_step, BLOCK, columns), incoming.dtype),
                pltpu.SemaphoreType.DMA((depth, per_step * n_data)),
            ],
        ),
        out_shape=[
            jax.ShapeDtypeStruct((slot_count, BLOCK, columns), incoming.dtype),
            jax.ShapeDtypeStruct((slot_count, BLOCK, sketch_width), jnp.float32),
        ],
        compiler_params=pltpu.CompilerParams(
            dimension_semantics=("arbitrary",), vmem_limit_bytes=32 * MIB
        ),
        name="finish",
    )(position, incoming, probe)


def shards(embed_rows, head_rows, row_offsets, slot_table, probe):
    n_tensor = lax.axis_size("tensor")
    n_data = lax.axis_size("dp")
    my_tensor = lax.axis_index("tensor")
    my_data = lax.axis_index("dp")
    quarter = R // 4
    height = embed_rows.shape[0]

    lead_part, trail_part = edges(row_offsets, embed_rows, head_rows, quarter)
    from_left = from_behind(trail_part, "tensor", 1)
    from_right = from_behind(lead_part, "tensor", -1)
    left = (my_tensor + n_tensor - 1) % n_tensor
    left_begin = tail_begin(row_offsets[:, left], left, height, quarter)
    skew = left_begin - floor_tile(left_begin)
    meta = jnp.stack(
        [row_offsets[:, my_tensor] - my_tensor * R, row_offsets[:, my_tensor + 1] - my_tensor * R, skew], axis=1
    )

    devices = n_tensor * n_data
    per_rank = R // BLOCK
    total_blocks = per_rank * n_tensor
    slot_count = 2 * total_blocks // devices
    max_from = slot_count // n_tensor
    slot_grid = slot_table.reshape(devices, slot_count)
    source = slot_grid % total_blocks // per_rank
    local_block = slot_grid // total_blocks * per_rank + slot_grid % per_rank
    from_me = source == my_tensor
    slot_range = jnp.arange(slot_count, dtype=jnp.int32)
    lower = slot_range[None, :] < slot_range[:, None]
    rank_order = jnp.sum((from_me[:, None, :] & lower[None]).astype(jnp.int32), axis=2)
    slot_index = jnp.arange(max_from, dtype=jnp.int32)
    select = from_me[:, None, :] & (rank_order[:, None, :] == slot_index[None, :, None])
    picked = jnp.sum(jnp.where(select, local_block[:, None, :], 0), axis=2).reshape(-1)
    writer = my_data * n_tensor + my_tensor
    my_source = source[writer]
    earlier = (my_source[None, :] == my_source[:, None]) & lower
    rank_within = jnp.sum(earlier.astype(jnp.int32), axis=1)
    data_range = jnp.arange(n_data, dtype=jnp.int32)
    position = (
        (data_range[None, :] * n_tensor + my_source[:, None]) * max_from + rank_within[:, None]
    ).reshape(-1)

    matrix = picked // per_rank
    first = picked % per_rank * BLOCK
    before = jnp.where(matrix == 0, meta[0, 0], meta[1, 0])
    after = jnp.where(matrix == 0, meta[0, 1], meta[1, 1])
    on_edge = (first < before) | (first + BLOCK > after)
    everything = jnp.arange(picked.shape[0], dtype=jnp.int32)
    turn = jnp.sum((on_edge[None, :] & (everything[None, :] < everything[:, None])).astype(jnp.int32), axis=1)
    most = jnp.arange(4 * quarter // BLOCK, dtype=jnp.int32)
    slots = jnp.sum(
        jnp.where(on_edge[None, :] & (turn[None, :] == most[:, None]), everything[None, :], 0), axis=1
    )
    count = jnp.sum(on_edge.astype(jnp.int32)).reshape(1)

    packed = pack(picked, meta, embed_rows, head_rows)
    outgoing = fix(slots, count, picked, meta, packed, from_left, from_right)
    incoming = lax.all_to_all(outgoing, ("dp", "tensor"), split_axis=0, concat_axis=0, tiled=True)
    stored, sketch = finish(position, incoming, probe, slot_count, n_data)
    return (stored, sketch)


def solution(mesh):
    return jax.shard_map(
        shards,
        mesh=mesh,
        in_specs=(P("tensor", "dp"), P("tensor", "dp"), P(), P(), P()),
        out_specs=(P(("dp", "tensor"), None, None), P(("dp", "tensor"), None, None)),
        check_vma=False,
    )
```

time: 180 us -> 157 us (0.87)
  Pallas kernels: 43.6 us -> 28.5 us
  waiting for transfers between devices: 114 us -> 104 us
  other arithmetic: 3.31 us -> 6.95 us
  starting transfers between devices: 14.1 us -> 11.3 us
  local copies, waits for them, and re-layouts: 2.88 us -> 4.88 us
    pallas_call x1, Pallas kernels: 28.3 us -> 4.61 us  [pack(): pl.pallas_call(functools.partial(pack_kernel, R // BLOCK, per_step), grid...]
    ppermute x2, waiting for transfers between devices: 20.6 us -> 10.9 us  [from_behind(): return lax.ppermute(block, axis, route)]
    pallas_call x0 -> x1, Pallas kernels: none -> 6.22 us  [fix(): pl.pallas_call(functools.partial(fix_kernel, R // BLOCK, group), grid_spe...]
    reduce_sum x0 -> x3, other arithmetic: none -> 3.29 us  [the longest x1 3.07 us: shards(): count = jnp.sum(on_edge.astype(jnp.int32)).reshape(1)]
    all_to_all x1, starting transfers between devices: 10.6 us -> 7.91 us  [shards(): lax.all_to_all(outgoing, ('dp', 'tensor'), split_axis=0, concat_axis=0, t...]
    or x0 -> x1, other arithmetic: none -> 2.42 us  [shards(): on_edge = (first < before) | (first + BLOCK > after)]
    pallas_call x1, Pallas kernels: 11.8 us -> 13.8 us  [finish(): pl.pallas_call(functools.partial(finish_kernel, n_data, per_step), grid_s...]
    unnamed x8 -> x12, local copies, waits for them, and re-layouts: 1.97 us -> 3.92 us
  transfers between devices with their start and end apart: 3 -> 3, of which waited for: 2 -> 3; matrix products, arithmetic and copies ran while one was open for 1% -> 5% of each run, Pallas kernels for 0% -> 3%
where the time goes in v2:
time: 157 us
  waiting for transfers between devices  104 us (66%)
  Pallas kernels  28.5 us (18%)
  starting transfers between devices  11.3 us (7%)
  other arithmetic  6.95 us (4%)
  local copies, waits for them, and re-layouts  4.88 us (3%)
    all_to_all x1, waiting for transfers between devices, shards(): lax.all_to_all(outgoing, ('dp', 'tensor'), split_axis=0, concat_axis=0, t...  93.3 us
    pallas_call x1, Pallas kernels, finish(): pl.pallas_call(functools.partial(finish_kernel, n_data, per_step), grid_s...  13.8 us
    ppermute x2, waiting for transfers between devices, from_behind(): return lax.ppermute(block, axis, route)  10.9 us
    all_to_all x1, starting transfers between devices, shards(): lax.all_to_all(outgoing, ('dp', 'tensor'), split_axis=0, concat_axis=0, t...  7.91 us
    pallas_call x1, Pallas kernels, fix(): pl.pallas_call(functools.partial(fix_kernel, R // BLOCK, group), grid_spe...  6.22 us
    pallas_call x1, Pallas kernels, pack(): pl.pallas_call(functools.partial(pack_kernel, R // BLOCK, per_step), grid...  4.61 us
    unnamed x12, local copies, waits for them, and re-layouts  3.92 us
    pallas_call x1, Pallas kernels, edges(): pl.pallas_call(edges_kernel, grid_spec=pltpu.PrefetchScalarGridSpec(num_s...  3.82 us
  transfers between devices with their start and end apart: 3, of which 3 were waited for; matrix products, arithmetic and copies ran while one was open for 5% of the time, Pallas kernels for 3%

profile of v2, /device:TPU:0, one launch (start us, length us, event | category | flops | bytes accessed | tf_op | source)
XLA Modules:
  0.0 156.6 jit_solution(5889582255609785563)
XLA Ops:
  0.7 3.8 %edges.1 = (bf16[2,2048,128]{2,1,0:T(8,128)(2,1)}, bf16[2,2064,128]{2,1,0:T(8,128)(2,1)}) custom-call(s32[2,9]{1,0:T(2,128)} %offsets_ref.1, bf16[12288,128]{1,0:T(8,128)(2,1)} %embed_ref.3, bf16[12288,128]{1,0:T(8,128)(2,1)} %head_ref.3), custom_call_target="tpu_custom_call" | custom-call | tf_op jit(solution)/shard_map/edges/pallas_call | solution.py:192
  4.5 3.4 %collective-permute-start.1 = (bf16[2,2048,128]{2,1,0:T(8,128)(2,1)}, bf16[2,2048,128]{2,1,0:T(8,128)(2,1)}, u32[]{:S(2)}, u32[]{:S(2)}) collective-permute-start(bf16[2,2048,128]{2,1,0:T(8,128)(2,1)} %get-tuple-element.5), channel_id=1, source_target_pairs={{1,0},{2,1},{3,2},{4,3},{5,4},{6,5},{7,6},{0,7},{9,8},{10,9},{11,1... | collective-permute-start | bytes 3145736 | tf_op jit(solution)/shard_map/ppermute | solution.py:20
  8.0 0.6 convert_reduce_fusion
  8.7 0.1 select_reduce_fusion
  8.8 0.1 copy.8
  8.9 0.1 reshape.206.picked_ref
  9.0 0.1 shift-left_subtract_fusion
  9.1 0.1 pad_add_fusion.meta_ref
  9.2 1.9 %copy-done.2 = bf16[12288,128]{1,0:T(8,128)(2,1)S(1)} copy-done((bf16[12288,128]{1,0:T(8,128)(2,1)S(1)}, bf16[12288,128]{1,0:T(8,128)(2,1)}, u32[]{:S(2)}) %copy-start.2) | copy-done | bytes 3145752
  11.1 4.6 %pack.1.packed_ref = bf16[128,128,128]{2,1,0:T(8,128)(2,1)S(1)} custom-call(s32[128]{0:T(128)S(1)} %reshape.206.picked_ref, s32[2,3]{1,0:T(2,128)S(1)} %pad_add_fusion.meta_ref, bf16[12288,128]{1,0:T(8,128)(2,1)S(1)} %copy-done.1, bf16[12288,128]{1,0:T(8,128)(2,1)S(1)} %copy-done.2), custom_call_target="tpu_custom_call" | custom-call | flops 1073741824 | bytes 25165824 | tf_op jit(solution)/shard_map/pack/pallas_call | solution.py:214
  15.7 0.6 fusion.16
  16.3 3.1 %convert_reduce_fusion.3 = s32[]{:T(128)} fusion(s32[32,4]{0,1:T(4,128)S(1)} %select_reduce_fusion, s32[]{:T(128)} %bitcast.4, s32[]{:T(128)} %bitcast.3, s32[]{:T(128)} %bitcast.2, s32[]{:T(128)} %bitcast.1), kind=kLoop, calls=%fused_computation.41 | loop fusion | flops 3711 | bytes 532 | tf_op jit(solution)/shard_map/reduce_sum | solution.py:348
  19.4 2.4 %compare_or_fusion = pred[128]{0:T(512)(128)(4,1)S(1)} fusion(s32[128]{0:T(128)S(1)} %reshape.206.picked_ref, s32[]{:T(128)} %bitcast.4, s32[]{:T(128)} %bitcast.3, s32[]{:T(128)} %bitcast.2, s32[]{:T(128)} %bitcast.1), kind=kLoop, calls=%fused_computation.47 | loop fusion | flops 3456 | bytes 656 | tf_op jit(solution)/shard_map/or | solution.py:341
  21.8 0.1 convert_reduce_fusion.1
  21.9 0.1 select_reduce_fusion.1.slots_ref
  22.0 8.9 %collective-permute-done.1.right_ref = bf16[2,2048,128]{2,1,0:T(8,128)(2,1)} collective-permute-done((bf16[2,2048,128]{2,1,0:T(8,128)(2,1)}, bf16[2,2048,128]{2,1,0:T(8,128)(2,1)}, u32[]{:S(2)}, u32[]{:S(2)}) %collective-permute-start.1) | collective-permute-done | bytes 1048608 | tf_op jit(solution)/shard_map/ppermute | solution.py:20
  31.0 1.9 %collective-permute-done.left_ref = bf16[2,2064,128]{2,1,0:T(8,128)(2,1)} collective-permute-done((bf16[2,2064,128]{2,1,0:T(8,128)(2,1)}, bf16[2,2064,128]{2,1,0:T(8,128)(2,1)}, u32[]{:S(2)}, u32[]{:S(2)}) %collective-permute-start) | collective-permute-done | bytes 1056800 | tf_op jit(solution)/shard_map/ppermute | solution.py:20
  32.9 6.2 %fix.1 = bf16[128,128,128]{2,1,0:T(8,128)(2,1)S(1)} custom-call(s32[64]{0:T(128)S(1)} %select_reduce_fusion.1.slots_ref, s32[1]{0:T(128)} %bitcast.5.count_ref, s32[128]{0:T(128)S(1)} %reshape.206.picked_ref, s32[2,3]{1,0:T(2,128)S(1)} %pad_add_fusion.meta_ref, bf16[128,128,128]{2,1,0:T(8,128)(2,1)S(1)} %pack.1.packed_ref, ...), custom_call_target="tpu_custom_call", output_to_operand_aliasing={{}: (4, {})} | custom-call | tf_op jit(solution)/shard_map/fix/pallas_call | solution.py:239
  39.1 2.0 %copy-done = bf16[128,128,128]{2,1,0:T(8,128)(2,1)} copy-done((bf16[128,128,128]{2,1,0:T(8,128)(2,1)}, bf16[128,128,128]{2,1,0:T(8,128)(2,1)S(1)}, u32[]{:S(2)}) %copy-start) | copy-done | bytes 4194328
  41.1 7.9 %all-to-all-start = ((bf16[128,128,128]{2,1,0:T(8,128)(2,1)}), bf16[128,128,128]{2,1,0:T(8,128)(2,1)}, u32[]{:S(2)}, u32[]{:S(2)}) async-start(bf16[128,128,128]{2,1,0:T(8,128)(2,1)} %copy-done), calls=%async_computation | async-start | bytes 8388608 | tf_op jit(solution)/shard_map/all_to_all | solution.py:352
  49.1 0.2 convert_reduce_fusion.2
  49.3 0.1 add.133.position_ref
  49.5 93.3 %all-to-all-done.incoming_ref = bf16[128,128,128]{2,1,0:T(8,128)(2,1)} async-done(((bf16[128,128,128]{2,1,0:T(8,128)(2,1)}), bf16[128,128,128]{2,1,0:T(8,128)(2,1)}, u32[]{:S(2)}, u32[]{:S(2)}) %all-to-all-start) | async-done | bytes 4194336 | tf_op jit(solution)/shard_map/all_to_all | solution.py:352
  142.7 13.8 %finish.1 = (bf16[32,128,512]{2,1,0:T(8,128)(2,1)}, f32[32,128,1024]{2,1,0:T(8,128)}) custom-call(s32[128]{0:T(128)S(1)} %add.133.position_ref, bf16[128,128,128]{2,1,0:T(8,128)(2,1)} %all-to-all-done.incoming_ref, bf16[512,1024]{1,0:T(8,128)(2,1)S(1)} %copy-done.3), custom_call_target="tpu_custom_call" | custom-call | tf_op jit(solution)/shard_map/finish/pallas_call | solution.py:266
  (17 shorter events, 0.2 us)
Async XLA Ops:
  0.6 8.4 %copy-start.4 = (s32[2,9]{1,0:T(2,128)S(1)}, s32[2,9]{1,0:T(2,128)}, u32[]{:S(2)}) copy-start(s32[2,9]{1,0:T(2,128)} %offsets_ref.1) | copy-start | bytes 220
  0.6 8.6 %copy-start.1 = (bf16[12288,128]{1,0:T(8,128)(2,1)S(1)}, bf16[12288,128]{1,0:T(8,128)(2,1)}, u32[]{:S(2)}) copy-start(bf16[12288,128]{1,0:T(8,128)(2,1)} %embed_ref.3) | copy-start | bytes 9437188
  0.6 7.3 %copy-start.5 = (s32[1024]{0:T(1024)S(1)}, s32[1024]{0:T(1024)}, u32[]{:S(2)}) copy-start(s32[1024]{0:T(1024)} %param.8) | copy-start | bytes 12292
  4.5 26.5 %collective-permute-start.1 = (bf16[2,2048,128]{2,1,0:T(8,128)(2,1)}, bf16[2,2048,128]{2,1,0:T(8,128)(2,1)}, u32[]{:S(2)}, u32[]{:S(2)}) collective-permute-start(bf16[2,2048,128]{2,1,0:T(8,128)(2,1)} %get-tuple-element.5), channel_id=1, source_target_pairs={{1,0},{2,1},{3,2},{4,3},{5,4},{6,5},{7,6},{0,7},{9,8},{10,9},{11,1... | collective-permute-start | bytes 3145736 | tf_op jit(solution)/shard_map/ppermute | solution.py:20
  7.9 25.0 %collective-permute-start = (bf16[2,2064,128]{2,1,0:T(8,128)(2,1)}, bf16[2,2064,128]{2,1,0:T(8,128)(2,1)}, u32[]{:S(2)}, u32[]{:S(2)}) collective-permute-start(bf16[2,2064,128]{2,1,0:T(8,128)(2,1)} %get-tuple-element.4), channel_id=1, source_target_pairs={{7,0},{0,1},{1,2},{2,3},{3,4},{4,5},{5,6},{6,7},{15,8},{8,9},{9,10... | collective-permute-start | bytes 3170312 | tf_op jit(solution)/shard_map/ppermute | solution.py:20
  9.2 1.9 %copy-start.2 = (bf16[12288,128]{1,0:T(8,128)(2,1)S(1)}, bf16[12288,128]{1,0:T(8,128)(2,1)}, u32[]{:S(2)}) copy-start(bf16[12288,128]{1,0:T(8,128)(2,1)} %head_ref.3) | copy-start | bytes 9437188
  39.1 2.0 %copy-start = (bf16[128,128,128]{2,1,0:T(8,128)(2,1)}, bf16[128,128,128]{2,1,0:T(8,128)(2,1)S(1)}, u32[]{:S(2)}) copy-start(bf16[128,128,128]{2,1,0:T(8,128)(2,1)S(1)} %fix.1) | copy-start | bytes 12582916
  41.1 101.6 %copy-start.3 = (bf16[512,1024]{1,0:T(8,128)(2,1)S(1)}, bf16[512,1024]{1,0:T(8,128)(2,1)}, u32[]{:S(2)}) copy-start(bf16[512,1024]{1,0:T(8,128)(2,1)} %probe_ref.1) | copy-start | bytes 3145732
  41.1 101.6 %all-to-all-start = ((bf16[128,128,128]{2,1,0:T(8,128)(2,1)}), bf16[128,128,128]{2,1,0:T(8,128)(2,1)}, u32[]{:S(2)}, u32[]{:S(2)}) async-start(bf16[128,128,128]{2,1,0:T(8,128)(2,1)} %copy-done), calls=%async_computation | async-start | bytes 8388608 | tf_op jit(solution)/shard_map/all_to_all | solution.py:352

commit v3 on v2

--- a/solution.py
+++ b/solution.py
@@ -86,25 +86,22 @@
 
 
 def fix_kernel(per_rank, group, slots_ref, count_ref, picked_ref, meta_ref, packed_ref, left_ref, right_ref,
-               out_ref, work, get_sems, put_sems):
-    del packed_ref
+               out_ref, work, sems):
     count = count_ref[0]
-
-    def get(k):
-        return pltpu.make_async_copy(out_ref.at[slots_ref[k]], work.at[k], get_sems.at[k])
+    total = out_ref.shape[0]
+
+    def keep(k):
+        return pltpu.make_async_copy(packed_ref.at[slots_ref[k]], out_ref.at[slots_ref[k]], sems.at[k])
 
     def put(k):
-        return pltpu.make_async_copy(work.at[k], out_ref.at[slots_ref[k]], put_sems.at[k])
-
-    def span(g):
-        return g * group, jnp.minimum(count, (g + 1) * group)
-
-    def start_get(k, carry):
-        get(k).start()
-        return carry
-
-    def wait_get(k, carry):
-        get(k).wait()
+        return pltpu.make_async_copy(work.at[k], out_ref.at[slots_ref[k]], sems.at[k])
+
+    def start_keep(k, carry):
+        keep(k).start()
+        return carry
+
+    def wait_keep(k, carry):
+        keep(k).wait()
         return carry
 
     def start_put(k, carry):
@@ -115,12 +112,10 @@
         put(k).wait()
         return carry
 
-    lax.fori_loop(0, count, start_get, 0)
+    lax.fori_loop(count, total, start_keep, 0)
     row = lax.broadcasted_iota(jnp.int32, (BLOCK, work.shape[2]), 0)
 
     def one_group(g, carry):
-        low_k, high_k = span(g)
-        lax.fori_loop(low_k, high_k, wait_get, 0)
         for q in range(group):
             k = g * group + q
             block = picked_ref[slots_ref[k]]
@@ -139,50 +134,26 @@
             low = jnp.where(is_left, 0, after - first)
             high = jnp.where(is_left, before - first, BLOCK)
             moved = jnp.dot(selector(offset), window, preferred_element_type=jnp.float32)
-            kept = work[k].astype(jnp.float32)
+            kept = packed_ref[slots_ref[k]].astype(jnp.float32)
             work[k] = jnp.where((row >= low) & (row < high), moved, kept).astype(work.dtype)
-        lax.fori_loop(low_k, high_k, start_put, 0)
+        lax.fori_loop(g * group, jnp.minimum(count, (g + 1) * group), start_put, 0)
         return carry
 
     lax.fori_loop(0, (count + group - 1) // group, one_group, 0)
     lax.fori_loop(0, count, wait_put, 0)
-
-
-def finish_kernel(n_data, per_step, position_ref, incoming_ref, probe_ref, stored_ref, sketch_ref, slots, sems):
+    lax.fori_loop(count, total, wait_keep, 0)
+
+
+def finish_kernel(n_data, per_step, position_ref, incoming_ref, probe_ref, stored_ref, sketch_ref):
     width = incoming_ref.shape[2]
     step = pl.program_id(0)
-    steps = pl.num_programs(0)
-    depth = slots.shape[0]
-
-    def copies(s):
-        place_of = lax.rem(s, depth)
-        return [
-            pltpu.make_async_copy(
-                incoming_ref.at[position_ref[(s * per_step + q) * n_data + d]],
-                slots.at[place_of, q, :, pl.ds(d * width, width)],
-                sems.at[place_of, q * n_data + d],
-            )
-            for q in range(per_step)
-            for d in range(n_data)
-        ]
-
-    @pl.when(step == 0)
-    def _():
-        for s in range(depth - 1):
-            for copy in copies(s):
-                copy.start()
-
-    @pl.when(step + depth - 1 < steps)
-    def _():
-        for copy in copies(step + depth - 1):
-            copy.start()
-
-    for copy in copies(step):
-        copy.wait()
-    here = lax.rem(step, depth)
     for q in range(per_step):
-        stored_ref[q] = slots[here, q]
-        sketch_ref[q] = jnp.dot(slots[here, q], probe_ref[...], preferred_element_type=jnp.float32)
+        for d in range(n_data):
+            where = position_ref[(step * per_step + q) * n_data + d]
+            stored_ref[q, :, d * width : (d + 1) * width] = incoming_ref[where]
+    rows = stored_ref[...].reshape(per_step * BLOCK, n_data * width)
+    product = jnp.dot(rows, probe_ref[...], preferred_element_type=jnp.float32)
+    sketch_ref[...] = product.reshape(sketch_ref.shape)
 
 
 def edges(row_offsets, embed_rows, head_rows, quarter):
@@ -235,50 +206,44 @@
 
 
 def fix(slots, count, picked, meta, packed, from_left, from_right):
-    most, group = slots.shape[0], 8
+    most, group = 4 * (R // 4) // BLOCK, 8
     return pl.pallas_call(
         functools.partial(fix_kernel, R // BLOCK, group),
         grid_spec=pltpu.PrefetchScalarGridSpec(
             num_scalar_prefetch=4,
             grid=(),
             in_specs=[
-                pl.BlockSpec(memory_space=pltpu.HBM),
                 pl.BlockSpec(memory_space=pltpu.VMEM),
                 pl.BlockSpec(memory_space=pltpu.VMEM),
-            ],
-            out_specs=pl.BlockSpec(memory_space=pltpu.HBM),
+                pl.BlockSpec(memory_space=pltpu.VMEM),
+            ],
+            out_specs=pl.BlockSpec(memory_space=pl.ANY),
             scratch_shapes=[
                 pltpu.VMEM((most,) + packed.shape[1:], packed.dtype),
-                pltpu.SemaphoreType.DMA((most,)),
-                pltpu.SemaphoreType.DMA((most,)),
+                pltpu.SemaphoreType.DMA((packed.shape[0],)),
             ],
         ),
         out_shape=jax.ShapeDtypeStruct(packed.shape, packed.dtype),
-        input_output_aliases={4: 0},
-        compiler_params=pltpu.CompilerParams(vmem_limit_bytes=24 * MIB),
+        compiler_params=pltpu.CompilerParams(vmem_limit_bytes=57 * MIB),
         name="fix",
     )(slots, count, picked, meta, packed, from_left, from_right)
 
 
 def finish(position, incoming, probe, slot_count, n_data):
     columns, sketch_width = probe.shape
-    per_step, depth = 2, 4
+    per_step = 4
     return pl.pallas_call(
         functools.partial(finish_kernel, n_data, per_step),
         grid_spec=pltpu.PrefetchScalarGridSpec(
             num_scalar_prefetch=1,
             grid=(slot_count // per_step,),
             in_specs=[
-                pl.BlockSpec(memory_space=pl.ANY),
+                pl.BlockSpec(incoming.shape, lambda i, *_: (0, 0, 0)),
                 pl.BlockSpec(probe.shape, lambda i, *_: (0, 0)),
             ],
             out_specs=[
                 pl.BlockSpec((per_step, BLOCK, columns), lambda i, *_: (i, 0, 0)),
                 pl.BlockSpec((per_step, BLOCK, sketch_width), lambda i, *_: (i, 0, 0)),
-            ],
-            scratch_shapes=[
-                pltpu.VMEM((depth, per_step, BLOCK, columns), incoming.dtype),
-                pltpu.SemaphoreType.DMA((depth, per_step * n_data)),
             ],
         ),
         out_shape=[
@@ -286,7 +251,7 @@
             jax.ShapeDtypeStruct((slot_count, BLOCK, sketch_width), jnp.float32),
         ],
         compiler_params=pltpu.CompilerParams(
-            dimension_semantics=("arbitrary",), vmem_limit_bytes=32 * MIB
+            dimension_semantics=("arbitrary",), vmem_limit_bytes=48 * MIB
         ),
         name="finish",
     )(position, incoming, probe)
@@ -340,12 +305,10 @@
     after = jnp.where(matrix == 0, meta[0, 1], meta[1, 1])
     on_edge = (first < before) | (first + BLOCK > after)
     everything = jnp.arange(picked.shape[0], dtype=jnp.int32)
-    turn = jnp.sum((on_edge[None, :] & (everything[None, :] < everything[:, None])).astype(jnp.int32), axis=1)
-    most = jnp.arange(4 * quarter // BLOCK, dtype=jnp.int32)
-    slots = jnp.sum(
-        jnp.where(on_edge[None, :] & (turn[None, :] == most[:, None]), everything[None, :], 0), axis=1
-    )
+    ahead = jnp.sum((on_edge[None, :] & (everything[None, :] < everything[:, None])).astype(jnp.int32), axis=1)
     count = jnp.sum(on_edge.astype(jnp.int32)).reshape(1)
+    turn = jnp.where(on_edge, ahead, count + everything - ahead)
+    slots = jnp.sum(jnp.where(turn[None, :] == everything[:, None], everything[None, :], 0), axis=1)
 
     packed = pack(picked, meta, embed_rows, head_rows)
     outgoing = fix(slots, count, picked, meta, packed, from_left, from_right)

time: 157 us -> 152 us (0.968)
  waiting for transfers between devices: 104 us -> 98.5 us
  other arithmetic: 6.95 us -> 10.5 us
  starting transfers between devices: 11.3 us -> 8.92 us
    ppermute x2, waiting for transfers between devices: 10.9 us -> 5.24 us  [from_behind(): return lax.ppermute(block, axis, route)]
    select_n x0 -> x1, other arithmetic: none -> 3.03 us  [shards(): turn = jnp.where(on_edge, ahead, count + everything - ahead)]
    all_to_all x1, starting transfers between devices: 7.91 us -> 5.5 us  [shards(): lax.all_to_all(outgoing, ('dp', 'tensor'), split_axis=0, concat_axis=0, t...]
    pallas_call x1, Pallas kernels: 6.22 us -> 8.28 us  [fix(): pl.pallas_call(functools.partial(fix_kernel, R // BLOCK, group), grid_spe...]
    pallas_call x1, Pallas kernels: 13.8 us -> 11.8 us  [finish(): pl.pallas_call(functools.partial(finish_kernel, n_data, per_step), grid_s...]
    unnamed x12 -> x16, local copies, waits for them, and re-layouts: 3.92 us -> 3.92 us
  transfers between devices with their start and end apart: 3 -> 3, of which waited for: 3 -> 3; matrix products, arithmetic and copies ran while one was open for 5% -> 8% of each run, Pallas kernels for 3% -> 3%
where the time goes in v3:
time: 152 us
  waiting for transfers between devices  98.5 us (65%)
  Pallas kernels  28.5 us (19%)
  other arithmetic  10.5 us (7%)
  starting transfers between devices  8.92 us (6%)
  local copies, waits for them, and re-layouts  4.9 us (3%)
    all_to_all x1, waiting for transfers between devices, shards(): lax.all_to_all(outgoing, ('dp', 'tensor'), split_axis=0, concat_axis=0, t...  93.3 us
    pallas_call x1, Pallas kernels, finish(): pl.pallas_call(functools.partial(finish_kernel, n_data, per_step), grid_s...  11.8 us
    pallas_call x1, Pallas kernels, fix(): pl.pallas_call(functools.partial(fix_kernel, R // BLOCK, group), grid_spe...  8.28 us
    all_to_all x1, starting transfers between devices, shards(): lax.all_to_all(outgoing, ('dp', 'tensor'), split_axis=0, concat_axis=0, t...  5.5 us
    ppermute x2, waiting for transfers between devices, from_behind(): return lax.ppermute(block, axis, route)  5.24 us
    pallas_call x1, Pallas kernels, pack(): pl.pallas_call(functools.partial(pack_kernel, R // BLOCK, per_step), grid...  4.6 us
    unnamed x16, local copies, waits for them, and re-layouts  3.92 us
    pallas_call x1, Pallas kernels, edges(): pl.pallas_call(edges_kernel, grid_spec=pltpu.PrefetchScalarGridSpec(num_s...  3.82 us
  transfers between devices with their start and end apart: 3, of which 3 were waited for; matrix products, arithmetic and copies ran while one was open for 8% of the time, Pallas kernels for 3%

profile of v3, /device:TPU:0, one launch (start us, length us, event | category | flops | bytes accessed | tf_op | source)
XLA Modules:
  0.0 152.2 jit_solution(3573465903058682021)
XLA Ops:
  0.7 3.8 %edges.1 = (bf16[2,2048,128]{2,1,0:T(8,128)(2,1)}, bf16[2,2064,128]{2,1,0:T(8,128)(2,1)}) custom-call(s32[2,9]{1,0:T(2,128)} %offsets_ref.1, bf16[12288,128]{1,0:T(8,128)(2,1)} %embed_ref.3, bf16[12288,128]{1,0:T(8,128)(2,1)} %head_ref.3), custom_call_target="tpu_custom_call" | custom-call | tf_op jit(solution)/shard_map/edges/pallas_call | solution.py:163
  4.5 3.4 %collective-permute-start.1 = (bf16[2,2048,128]{2,1,0:T(8,128)(2,1)}, bf16[2,2048,128]{2,1,0:T(8,128)(2,1)}, u32[]{:S(2)}, u32[]{:S(2)}) collective-permute-start(bf16[2,2048,128]{2,1,0:T(8,128)(2,1)} %get-tuple-element.5), channel_id=1, source_target_pairs={{1,0},{2,1},{3,2},{4,3},{5,4},{6,5},{7,6},{0,7},{9,8},{10,9},{11,1... | collective-permute-start | bytes 3145736 | tf_op jit(solution)/shard_map/ppermute | solution.py:20
  8.0 0.6 convert_reduce_fusion
  8.7 0.1 select_reduce_fusion.1
  8.8 0.1 shift-left_subtract_fusion
  9.0 0.1 copy.7
  9.1 0.1 reshape.229.picked_ref
  9.2 1.9 %copy-done.2 = bf16[12288,128]{1,0:T(8,128)(2,1)S(1)} copy-done((bf16[12288,128]{1,0:T(8,128)(2,1)S(1)}, bf16[12288,128]{1,0:T(8,128)(2,1)}, u32[]{:S(2)}) %copy-start.2) | copy-done | bytes 3145752
  11.1 4.6 %pack.1.packed_ref = bf16[128,128,128]{2,1,0:T(8,128)(2,1)S(1)} custom-call(s32[128]{0:T(128)S(1)} %reshape.229.picked_ref, s32[2,3]{1,0:T(2,128)S(1)} %pad_add_fusion.meta_ref, bf16[12288,128]{1,0:T(8,128)(2,1)S(1)} %copy-done.1, bf16[12288,128]{1,0:T(8,128)(2,1)S(1)} %copy-done.2), custom_call_target="tpu_custom_call" | custom-call | flops 1073741824 | bytes 25165824 | tf_op jit(solution)/shard_map/pack/pallas_call | solution.py:185
  15.7 2.0 %copy-done = bf16[128,128,128]{2,1,0:T(8,128)(2,1)} copy-done((bf16[128,128,128]{2,1,0:T(8,128)(2,1)}, bf16[128,128,128]{2,1,0:T(8,128)(2,1)S(1)}, u32[]{:S(2)}) %copy-start) | copy-done | bytes 4194328
  17.7 0.6 fusion.15
  18.3 3.1 %convert_reduce_fusion.3 = s32[]{:T(128)} fusion(s32[32,4]{0,1:T(4,128)S(1)} %select_reduce_fusion.1, s32[]{:T(128)} %bitcast.4, s32[]{:T(128)} %bitcast.3, s32[]{:T(128)} %bitcast.2, s32[]{:T(128)} %bitcast.1), kind=kLoop, calls=%fused_computation.40 | loop fusion | flops 3711 | bytes 532 | tf_op jit(solution)/shard_map/reduce_sum | solution.py:309
  21.4 2.5 %compare_or_fusion = pred[128]{0:T(512)(128)(4,1)S(1)} fusion(s32[128]{0:T(128)S(1)} %reshape.229.picked_ref, s32[]{:T(128)} %bitcast.4, s32[]{:T(128)} %bitcast.3, s32[]{:T(128)} %bitcast.2, s32[]{:T(128)} %bitcast.1), kind=kLoop, calls=%fused_computation.46 | loop fusion | flops 3456 | bytes 656 | tf_op jit(solution)/shard_map/or | solution.py:306
  23.9 0.1 convert_reduce_fusion.1
  24.0 3.0 %subtract_select_fusion = s32[128]{0:T(128)S(1)} fusion(s32[128]{0:T(128)S(1)} %convert_reduce_fusion.1, s32[]{:T(128)} %convert_reduce_fusion.3, s32[]{:T(128)} %bitcast.4, s32[]{:T(128)} %bitcast.3, s32[]{:T(128)} %bitcast.2, s32[]{:T(128)} %bitcast.1, s32[128]{0:T(128)S(1)} %reshape.229.picked_ref), kind=kLoop, calls=%fused_computation.59 | loop fusion | flops 3840 | bytes 1556 | tf_op jit(solution)/shard_map/jit(_where)/select_n | solution.py:310
  27.0 0.6 select_reduce_fusion.slots_ref
  27.6 3.3 %collective-permute-done.1.right_ref = bf16[2,2048,128]{2,1,0:T(8,128)(2,1)} collective-permute-done((bf16[2,2048,128]{2,1,0:T(8,128)(2,1)}, bf16[2,2048,128]{2,1,0:T(8,128)(2,1)}, u32[]{:S(2)}, u32[]{:S(2)}) %collective-permute-start.1) | collective-permute-done | bytes 1048608 | tf_op jit(solution)/shard_map/ppermute | solution.py:20
  31.0 1.9 %collective-permute-done.left_ref = bf16[2,2064,128]{2,1,0:T(8,128)(2,1)} collective-permute-done((bf16[2,2064,128]{2,1,0:T(8,128)(2,1)}, bf16[2,2064,128]{2,1,0:T(8,128)(2,1)}, u32[]{:S(2)}, u32[]{:S(2)}) %collective-permute-start) | collective-permute-done | bytes 1056800 | tf_op jit(solution)/shard_map/ppermute | solution.py:20
  32.9 8.3 %fix.1 = bf16[128,128,128]{2,1,0:T(8,128)(2,1)} custom-call(s32[128]{0:T(128)} %select_reduce_fusion.slots_ref, s32[1]{0:T(128)} %bitcast.5.count_ref, s32[128]{0:T(128)} %copy-done.4, s32[2,3]{1,0:T(2,128)} %copy-done.5, bf16[128,128,128]{2,1,0:T(8,128)(2,1)} %copy-done, bf16[2,2064,128]{2,1,0:T(8,128)(2,1)} %collective-permute-done.left_ref, ...), custom_call_target="tpu_custom_call" | custom-call | tf_op jit(solution)/shard_map/fix/pallas_call | solution.py:210
  41.2 5.5 %all-to-all-start = ((bf16[128,128,128]{2,1,0:T(8,128)(2,1)}), bf16[128,128,128]{2,1,0:T(8,128)(2,1)}, u32[]{:S(2)}, u32[]{:S(2)}) async-start(bf16[128,128,128]{2,1,0:T(8,128)(2,1)} %fix.1), calls=%async_computation | async-start | bytes 8388608 | tf_op jit(solution)/shard_map/all_to_all | solution.py:315
  46.7 0.2 convert_reduce_fusion.2
  47.0 0.1 add.154.position_ref
  47.1 93.3 %all-to-all-done.incoming_ref = bf16[128,128,128]{2,1,0:T(8,128)(2,1)} async-done(((bf16[128,128,128]{2,1,0:T(8,128)(2,1)}), bf16[128,128,128]{2,1,0:T(8,128)(2,1)}, u32[]{:S(2)}, u32[]{:S(2)}) %all-to-all-start) | async-done | bytes 4194336 | tf_op jit(solution)/shard_map/all_to_all | solution.py:315
  140.4 11.8 %finish.1 = (bf16[32,128,512]{2,1,0:T(8,128)(2,1)}, f32[32,128,1024]{2,1,0:T(8,128)}) custom-call(s32[128]{0:T(128)S(1)} %add.154.position_ref, bf16[128,128,128]{2,1,0:T(8,128)(2,1)} %all-to-all-done.incoming_ref, bf16[512,1024]{1,0:T(8,128)(2,1)S(1)} %copy-done.3), custom_call_target="tpu_custom_call" | custom-call | tf_op jit(solution)/shard_map/finish/pallas_call | solution.py:235
  (22 shorter events, 0.3 us)
Async XLA Ops:
  0.6 8.2 %copy-start.6 = (s32[2,9]{1,0:T(2,128)S(1)}, s32[2,9]{1,0:T(2,128)}, u32[]{:S(2)}) copy-start(s32[2,9]{1,0:T(2,128)} %offsets_ref.1) | copy-start | bytes 220
  0.6 8.6 %copy-start.1 = (bf16[12288,128]{1,0:T(8,128)(2,1)S(1)}, bf16[12288,128]{1,0:T(8,128)(2,1)}, u32[]{:S(2)}) copy-start(bf16[12288,128]{1,0:T(8,128)(2,1)} %embed_ref.3) | copy-start | bytes 9437188
  0.6 7.3 %copy-start.7 = (s32[1024]{0:T(1024)S(1)}, s32[1024]{0:T(1024)}, u32[]{:S(2)}) copy-start(s32[1024]{0:T(1024)} %param.8) | copy-start | bytes 12292
  4.5 26.5 %collective-permute-start.1 = (bf16[2,2048,128]{2,1,0:T(8,128)(2,1)}, bf16[2,2048,128]{2,1,0:T(8,128)(2,1)}, u32[]{:S(2)}, u32[]{:S(2)}) collective-permute-start(bf16[2,2048,128]{2,1,0:T(8,128)(2,1)} %get-tuple-element.5), channel_id=1, source_target_pairs={{1,0},{2,1},{3,2},{4,3},{5,4},{6,5},{7,6},{0,7},{9,8},{10,9},{11,1... | collective-permute-start | bytes 3145736 | tf_op jit(solution)/shard_map/ppermute | solution.py:20
  7.9 25.0 %collective-permute-start = (bf16[2,2064,128]{2,1,0:T(8,128)(2,1)}, bf16[2,2064,128]{2,1,0:T(8,128)(2,1)}, u32[]{:S(2)}, u32[]{:S(2)}) collective-permute-start(bf16[2,2064,128]{2,1,0:T(8,128)(2,1)} %get-tuple-element.4), channel_id=1, source_target_pairs={{7,0},{0,1},{1,2},{2,3},{3,4},{4,5},{5,6},{6,7},{15,8},{8,9},{9,10... | collective-permute-start | bytes 3170312 | tf_op jit(solution)/shard_map/ppermute | solution.py:20
  9.0 6.7 %copy-start.5 = (s32[2,3]{1,0:T(2,128)}, s32[2,3]{1,0:T(2,128)S(1)}, u32[]{:S(2)}) copy-start(s32[2,3]{1,0:T(2,128)S(1)} %pad_add_fusion.meta_ref) | copy-start | bytes 76
  9.2 1.9 %copy-start.2 = (bf16[12288,128]{1,0:T(8,128)(2,1)S(1)}, bf16[12288,128]{1,0:T(8,128)(2,1)}, u32[]{:S(2)}) copy-start(bf16[12288,128]{1,0:T(8,128)(2,1)} %head_ref.3) | copy-start | bytes 9437188
  11.1 12.9 %copy-start.4 = (s32[128]{0:T(128)}, s32[128]{0:T(128)S(1)}, u32[]{:S(2)}) copy-start(s32[128]{0:T(128)S(1)} %reshape.229.picked_ref) | copy-start | bytes 1540
  15.7 2.0 %copy-start = (bf16[128,128,128]{2,1,0:T(8,128)(2,1)}, bf16[128,128,128]{2,1,0:T(8,128)(2,1)S(1)}, u32[]{:S(2)}) copy-start(bf16[128,128,128]{2,1,0:T(8,128)(2,1)S(1)} %pack.1.packed_ref) | copy-start | bytes 12582916
  41.2 99.2 %copy-start.3 = (bf16[512,1024]{1,0:T(8,128)(2,1)S(1)}, bf16[512,1024]{1,0:T(8,128)(2,1)}, u32[]{:S(2)}) copy-start(bf16[512,1024]{1,0:T(8,128)(2,1)} %probe_ref.1) | copy-start | bytes 3145732
  41.2 99.2 %all-to-all-start = ((bf16[128,128,128]{2,1,0:T(8,128)(2,1)}), bf16[128,128,128]{2,1,0:T(8,128)(2,1)}, u32[]{:S(2)}, u32[]{:S(2)}) async-start(bf16[128,128,128]{2,1,0:T(8,128)(2,1)} %fix.1), calls=%async_computation | async-start | bytes 8388608 | tf_op jit(solution)/shard_map/all_to_all | solution.py:315
